TPU v7x, 8 devices: a whole 2x2x1 slice. The times are simulated.
8 devices in a mesh: dp: 1 (over z), ep: 8 (over x, y, core).
Axes of the slice: x: 2, y: 2, z: 1, core: 2. Of those that a mesh axis runs over, the one named last changes fastest.
Arguments:
- x: bfloat16 [1, 8, 256, 4096], P('dp', 'ep')
- expert: int32 [1, 8, 256, 8], P('dp', 'ep')
- slot: int32 [1, 8, 256, 8], P('dp', 'ep')
- gate: float32 [1, 8, 256, 8], P('dp', 'ep')
- w_gate: bfloat16 [64, 4096, 1408], P('ep')
- w_up: bfloat16 [64, 4096, 1408], P('ep')
- w_down: bfloat16 [64, 1408, 4096], P('ep')
- s_gate: bfloat16 [4096, 1408], replicated
- s_up: bfloat16 [4096, 1408], replicated
- s_down: bfloat16 [1408, 4096], replicated
Outputs:
- y: bfloat16 [1, 8, 256, 4096], P('dp', 'ep')
All inputs are finite; a program needn't handle non-finite values.
Results may differ from a plain program's by a relative error of at most 0.009.
Values are sent between devices in bfloat16 or wider.
A program may use at most 2 GiB of HBM per device.

v0:
```python
import jax
import jax.numpy as jnp
from jax import lax
from jax.sharding import NamedSharding, PartitionSpec as P


def einsum(form, a, b):
    return jnp.einsum(form, a.astype(jnp.float32), b.astype(jnp.float32))


def for_all(x, s_gate, s_up, s_down):
    h = jax.nn.silu(einsum("...d,df->...f", x, s_gate)) * einsum("...d,df->...f", x, s_up)
    return einsum("...f,fd->...d", h.astype(jnp.bfloat16), s_down)


def solution(mesh):
    def placed(v, *spec):
        return lax.with_sharding_constraint(v, NamedSharding(mesh, P(*spec)))

    def step(x, expert, slot, gate, w_gate, w_up, w_down, s_gate, s_up, s_down):
        experts, (tokens, top) = w_gate.shape[0], expert.shape[2:]
        slots = 5 * tokens * top // (4 * experts)
        to_expert = jax.nn.one_hot(expert, experts, dtype=jnp.bfloat16)
        to_slot = jax.nn.one_hot(slot, slots, dtype=jnp.bfloat16)
        weighted = to_expert * gate[..., None].astype(jnp.bfloat16)
        dispatch = einsum("abtke,abtkc->abtec", to_expert, to_slot).astype(jnp.bfloat16)
        combine = einsum("abtke,abtkc->abtec", weighted, to_slot).astype(jnp.bfloat16)
        z = einsum("abtec,abtd->aebcd", dispatch, x).astype(jnp.bfloat16)
        z = placed(z, "dp", None, "ep", None, None)
        z = placed(z, "dp", "ep", None, None, None)
        h = jax.nn.silu(einsum("aebcd,edf->aebcf", z, w_gate))
        h = (h * einsum("aebcd,edf->aebcf", z, w_up)).astype(jnp.bfloat16)
        out = einsum("aebcf,efd->aebcd", h, w_down).astype(jnp.bfloat16)
        out = placed(out, "dp", "ep", None, None, None)
        out = placed(out, "dp", None, "ep", None, None)
        y = einsum("abtec,aebcd->abtd", combine, out)
        return (y + for_all(x, s_gate, s_up, s_down)).astype(jnp.bfloat16)

    return step
```

profile of v0, /device:TPU:0, one launch (start us, length us, event | category | flops | bytes accessed | tf_op | source)
XLA Modules:
  0.0 671.6 jit_solution(13098318483734679493)
XLA Ops:
  0.0 0.0 copy-start
  0.0 1.0 copy.10
  1.0 0.0 copy-start.1
  1.0 0.8 copy.12
  1.8 0.0 copy-done.1
  1.8 0.0 copy-start.3
  1.9 0.6 copy-done.3
  2.5 3.6 convolution_convert_fusion.1
  6.1 5.6 copy.13
  11.8 0.0 copy-done
  11.8 9.9 %convolution_convert_fusion = bf16[64,40,4096]{2,1,0:T(8,128)(2,1)} fusion(bf16[256,64,40]{0,2,1:T(8,128)(2,1)S(1)} %copy.13, bf16[1,1,256,4096]{3,2,1,0:T(8,128)(2,1)S(1)} %copy-done), kind=kOutput, calls=%fused_computation.18 | convolution fusion | flops 5379194880 | bytes 24379392 | tf_op jit(solution)/abtec,abtd->aebcd/dot_general | solution.py:8
  21.7 236.3 %all-to-all.4 = bf16[1,8,8,1,40,4096]{5,4,2,3,0,1:T(8,128)(2,1)} all-to-all(bf16[1,8,8,1,40,4096]{5,4,2,3,0,1:T(8,128)(2,1)} %bitcast.137), channel_id=1, replica_groups=mesh['dp'=1,'ep'=8] {'ep'}, dimensions={1} | all-to-all | bytes 41943040 | tf_op jit(solution)/sharding_constraint;jit(solution)/sharding_constraint | solution.py:18
  258.0 50.2 %fusion.4 = f32[8,8,40,1408]{3,2,1,0:T(8,128)} fusion(bf16[8,4096,1408]{2,1,0:T(8,128)(2,1)} %param.4, bf16[1,8,8,1,40,4096]{5,4,2,3,0,1:T(8,128)(2,1)} %all-to-all.4), kind=kOutput, calls=%fused_computation.4 | convolution fusion | flops 29527900160 | bytes 127664128 | tf_op jit(solution)/aebcd,edf->aebcf/dot_general | solution.py:8
  308.2 49.7 %fusion.10 = bf16[1,8,8,40,1408]{4,3,2,1,0:T(8,128)(2,1)} fusion(f32[8,8,40,1408]{3,2,1,0:T(8,128)} %fusion.4, bf16[8,4096,1408]{2,1,0:T(8,128)(2,1)} %param.5, bf16[1,8,8,1,40,4096]{5,4,2,3,0,1:T(8,128)(2,1)} %all-to-all.4), kind=kOutput, calls=%fused_computation.12 | convolution fusion | flops 29549527040 | bytes 134873088 | tf_op jit(solution)/aebcd,edf->aebcf/dot_general | solution.py:8
  357.9 48.9 %convert_bitcast_fusion = bf16[1,8,8,1,40,4096]{5,4,2,1,3,0:T(8,128)(2,1)} fusion(bf16[8,1408,4096]{2,1,0:T(8,128)(2,1)} %param.6, bf16[1,8,8,40,1408]{4,3,2,1,0:T(8,128)(2,1)} %fusion.10), kind=kOutput, calls=%fused_computation.8 | convolution fusion | flops 29538385920 | bytes 120455168 | tf_op jit(solution)/aebcf,efd->aebcd/dot_general | solution.py:8
  406.8 17.5 %copy.16 = bf16[1,8,8,1,40,4096]{5,4,1,3,0,2:T(8,128)(2,1)} copy(bf16[1,8,8,1,40,4096]{5,4,2,1,3,0:T(8,128)(2,1)} %convert_bitcast_fusion) | data formatting | bytes 41943040 | tf_op jit(solution)/sharding_constraint;jit(solution)/sharding_constraint | solution.py:18
  424.3 0.0 copy-start.5
  424.3 0.0 copy-start.2
  424.3 0.0 copy-start.4
  424.3 5.2 all-to-all-start.1
  429.6 0.0 copy-done.5
  429.6 0.1 copy.11
  429.7 0.0 copy-done.2
  429.7 0.0 copy-done.4
  429.7 4.3 convolution_convert_fusion.2
  434.0 5.6 copy.23
  439.6 7.3 %convolution_bitcast_fusion.2 = f32[1,256,1408]{2,1,0:T(8,128)} fusion(bf16[4096,1408]{1,0:T(8,128)(2,1)} %param.7, bf16[1,1,256,4096]{3,2,1,0:T(8,128)(2,1)S(1)} %copy-done), kind=kOutput, calls=%fused_computation.26 | convolution fusion | flops 2952790016 | bytes 15073280 | tf_op jit(solution)/...d,df->...f/dot_general | solution.py:8
  447.0 16.7 %fusion.37 = f32[256,4096]{1,0:T(8,128)} fusion(bf16[1408,4096]{1,0:T(8,128)(2,1)} %param.9, bf16[4096,1408]{1,0:T(8,128)(2,1)} %param.8, bf16[1,1,256,4096]{3,2,1,0:T(8,128)(2,1)S(1)} %copy-done, f32[1,256,1408]{2,1,0:T(8,128)} %convolution_bitcast_fusion.2), kind=kOutput, calls=%fused_computation.39 | convolution fusion | flops 5907742720 | bytes 30801920 | tf_op jit(solution)/...f,fd->...d/dot_general | solution.py:8
  463.7 193.5 %all-to-all-done.1 = bf16[1,8,8,1,40,4096]{5,4,1,3,0,2:T(8,128)(2,1)} async-done(((bf16[1,8,8,1,40,4096]{5,4,1,3,0,2:T(8,128)(2,1)}), bf16[1,8,8,1,40,4096]{5,4,1,3,0,2:T(8,128)(2,1)}, u32[]{:S(2)}, u32[]{:S(2)}) %all-to-all-start.1) | async-done | bytes 20971552 | tf_op jit(solution)/sharding_constraint;jit(solution)/sharding_constraint | solution.py:18
  657.1 14.4 %fusion.23 = bf16[1,1,256,4096]{3,2,1,0:T(8,128)(2,1)} fusion(f32[256,4096]{1,0:T(8,128)} %fusion.37, bf16[256,64,40]{0,2,1:T(8,128)(2,1)S(1)} %copy.23, bf16[64,40,4096]{2,1,0:T(8,128)(2,1)} %bitcast.38), kind=kOutput, calls=%fused_computation.23 | convolution fusion | flops 5370806272 | bytes 28573696 | tf_op jit(solution)/abtec,aebcd->abtd/dot_general | solution.py:8
  (1 shorter events, 0.0 us)
Async XLA Ops:
  0.0 11.8 %copy-start = (bf16[1,1,256,4096]{3,2,1,0:T(8,128)(2,1)S(1)}, bf16[1,1,256,4096]{3,2,1,0:T(8,128)(2,1)}, u32[]{:S(2)}) copy-start(bf16[1,1,256,4096]{3,2,1,0:T(8,128)(2,1)} %param.3) | copy-start | bytes 6291460
  1.0 0.9 copy-start.1
  1.8 0.7 copy-start.3
  424.3 5.2 copy-start.5
  424.3 5.4 copy-start.2
  424.3 5.4 copy-start.4
  424.3 232.8 %all-to-all-start.1 = ((bf16[1,8,8,1,40,4096]{5,4,1,3,0,2:T(8,128)(2,1)}), bf16[1,8,8,1,40,4096]{5,4,1,3,0,2:T(8,128)(2,1)}, u32[]{:S(2)}, u32[]{:S(2)}) async-start(bf16[1,8,8,1,40,4096]{5,4,1,3,0,2:T(8,128)(2,1)} %copy.16), calls=%async_computation.1 | async-start | bytes 41943040 | tf_op jit(solution)/sharding_constraint;jit(solution)/sharding_constraint | solution.py:18
where the time goes:
time: 672 us
  blocking collectives  236 us (35%)
  matrix products  205 us (31%)
  waiting for transfers between devices  193 us (29%)
  local copies, waits for them, and re-layouts  31.3 us (5%)
    another operation x1, blocking collectives, placed(): return lax.with_sharding_constraint(v, NamedSharding(mesh, P(*spec)))  236 us
    dot_general x9, matrix products, einsum(): return jnp.einsum(form, a.astype(jnp.float32), b.astype(jnp.float32))  205 us
    another operation x1, waiting for transfers between devices, placed(): return lax.with_sharding_constraint(v, NamedSharding(mesh, P(*spec)))  193 us
    another operation x1, local copies, waits for them, and re-layouts, placed(): return lax.with_sharding_constraint(v, NamedSharding(mesh, P(*spec)))  17.5 us
  transfers between devices with their start and end apart: 1, of which 1 were waited for; matrix products, arithmetic and copies ran while one was open for 5% of the time, Pallas kernels for 0%

commit v1 on v0

v1 whole, which is shorter than its diff:
```python
import functools

import jax
import jax.numpy as jnp
from jax import lax
from jax.experimental import pallas as pl
from jax.experimental.pallas import tpu as pltpu
from jax.sharding import PartitionSpec as P

N = 8
T = 256
D = 4096
FF = 1408
EL = 8
SL = 40
R = EL * SL
EM = N * SL
ROWS = EL * EM
W = 256
KC = 512
NC = D // KC
NS = D // W
NT = 2 * FF // W
KT = 6
SLOT = 5632
NSLOT = 3
ITEMS1 = NC + NC * EL
PER2 = 5
ITEMS = ITEMS1 + NC * PER2

S1R = KT * ROWS
S2R = S1R + NC * 512
SIBR = S2R + NC * 1024
S1S = SIBR + 2 * 2048
XROWS = S1S + 2 * 512
YST = 2048
SHR = NC * 2048

f32, bf16 = jnp.float32, jnp.bfloat16


def dot(a, b):
    return jnp.dot(a, b, preferred_element_type=f32)


def kernel(x, info, wg, wu, wd, sg, su, sd, y, xbuf, acc, w, z, dm, cm, hsh, ssend, infos,
           wsem, xsem, is_, ir, ag_s, xy_r, dg_r, sb_r, sib_s, sib_r, s1_s, s1_r, s2_s, s2_r, ysem, credit, ready):
    me = lax.axis_index("ep")
    mx, my, mc = me // 4, (me // 2) % 2, me % 2
    dx = (1 - mx) * 4 + my * 2 + mc
    dy = mx * 4 + (1 - my) * 2 + mc
    dd = (1 - mx) * 4 + (1 - my) * 2 + mc
    ds = mx * 4 + my * 2 + (1 - mc)

    def rows(ref, start, n):
        return ref.at[pl.ds(pl.multiple_of(start, 8), n)]

    def ld(ref, start, n):
        return ref[pl.ds(pl.multiple_of(start, 8), n), :]

    def send(src, dst, ss, rs, dev):
        pltpu.make_async_remote_copy(
            src_ref=src, dst_ref=dst, send_sem=ss, recv_sem=rs,
            device_id={"ep": dev}, device_id_type=pl.DeviceIdType.MESH).start()

    def wait(ref, n, sem):
        v = ref.at[pl.ds(0, n)]
        pltpu.make_async_copy(v, v, sem).wait()

    def start_item(i):
        slot = i % NSLOT
        base = slot * SLOT
        sem = wsem.at[slot]

        def first(g, u, c):
            def put(src, c0, n, t, l0):
                pltpu.make_async_copy(
                    src.at[pl.ds(pl.multiple_of(c * KC, KC), KC), pl.ds(c0, n)],
                    w.at[pl.ds(pl.multiple_of(base + t * KC, KC), KC), pl.ds(l0, n)], sem).start()
            for t in range(5):
                put(g, t * W, W, t, 0)
            put(g, 5 * W, 128, 5, 0)
            put(u, 5 * W, 128, 5, 128)
            for t in range(5):
                put(u, t * W, W, 6 + t, 0)

        @pl.when(i < NC)
        def _():
            first(sg, su, i)

        @pl.when((i >= NC) & (i < ITEMS1))
        def _():
            k = i - NC
            first(wg.at[k % EL], wu.at[k % EL], k // EL)

        @pl.when((i >= ITEMS1) & (i < ITEMS))
        def _():
            k = i - ITEMS1
            c, j = k // PER2, k % PER2

            def put(src, h, t):
                pltpu.make_async_copy(
                    src.at[:, pl.ds(pl.multiple_of(c * KC + h * W, W), W)],
                    rows(w, base + t * FF, FF), sem).start()

            @pl.when(j < 4)
            def _():
                for ee in range(2):
                    for h in range(2):
                        put(wd.at[j * 2 + ee], h, ee * 2 + h)

            @pl.when(j == 4)
            def _():
                for h in range(2):
                    put(sd, h, h)

    def wait_item(i, n=SLOT):
        wait(w, n, wsem.at[i % NSLOT])
        return (i % NSLOT) * SLOT

    def xr(s, src, r0=0, n=T):
        return rows(xbuf, (s * N + src) * T + r0, n)

    def own_out(s):
        for dev, sem in ((dx, xy_r), (dy, xy_r), (ds, sb_r)):
            send(xr(s, me), xr(s, me), ag_s.at[s], sem.at[s], dev)

    def tick(k):
        @pl.when(k < NS)
        def _():
            wait(xbuf, 2 * T, xy_r.at[k])
            send(xr(k, dx, 0, 128), xr(k, dx, 0, 128), ag_s.at[k], dg_r.at[k], dy)
            send(xr(k, dy, 128, 128), xr(k, dy, 128, 128), ag_s.at[k], dg_r.at[k], dx)
            send(xr(k, dx), xr(k, dx), ag_s.at[k], sb_r.at[k], ds)
            send(xr(k, dy), xr(k, dy), ag_s.at[k], sb_r.at[k], ds)

        @pl.when(k + 2 < NS)
        def _():
            own_out(k + 2)

        @pl.when((k >= 1) & (k <= NS))
        def _():
            wait(xbuf, T, dg_r.at[k - 1])
            send(xr(k - 1, dd), xr(k - 1, dd), ag_s.at[k - 1], sb_r.at[k - 1], ds)

    for s in range(NS):
        pltpu.make_async_copy(x.at[:, pl.ds(s * W, W)], xr(s, me), xsem).start()
    for i in range(NSLOT):
        start_item(jnp.int32(i))
    barrier = pltpu.get_barrier_semaphore()
    for k in range(1, N):
        pl.semaphore_signal(barrier, inc=1, device_id={"ep": (me + k) % N}, device_id_type=pl.DeviceIdType.MESH)
    pl.semaphore_wait(barrier, N - 1)
    for k in range(1, N):
        send(info, rows(infos, me * 16, 16), is_, ir, (me + k) % N)
    wait(xbuf, NS * T, xsem)
    own_out(0)
    own_out(1)
    infos[pl.ds(pl.multiple_of(me * 16, 16), 16), :] = info[...]

    def shared_step(c, _):
        base = wait_item(c)
        lhs = jnp.concatenate([xr(2 * c, me)[...], xr(2 * c + 1, me)[...]], axis=1)
        for t in range(NT):
            r = dot(lhs, ld(w, base + t * KC, KC))
            at = pl.ds(t * ROWS, T)
            acc[at, :] = jnp.where(c > 0, acc[at, :], 0.0) + r
        start_item(c + NSLOT)

        @pl.when(c == 4)
        def _():
            tick(jnp.int32(0))
        return 0

    lax.fori_loop(0, NC, shared_step, 0)

    def act(g, u):
        return (g * (0.5 * jnp.tanh(0.5 * g) + 0.5) * u).astype(bf16)

    def hidden(g0, n, put):
        for t in range(5):
            put(t, act(ld(acc, t * ROWS + g0, n), ld(acc, (6 + t) * ROWS + g0, n)), W)
        v = ld(acc, 5 * ROWS + g0, n)
        put(5, act(v[:, :128], v[:, 128:]), 128)

    def put_shared(t, v, n):
        hsh[:, t * W:t * W + n] = v

    hidden(0, T, put_shared)
    tick(jnp.int32(1))

    wait(infos, 7 * 16, ir)
    wait(infos, 7 * 16, is_)
    base_row = (me * R).astype(f32)

    def tables(s, _):
        v = infos[pl.ds(pl.multiple_of(s * 16, 16), 16), :]
        rid = lax.broadcasted_iota(jnp.int32, (R, T), 0).astype(f32) + base_row
        m = rid == v[0:1, :]
        for j in range(1, 8):
            m = m | (rid == v[j:j + 1, :])
        dm[pl.ds(pl.multiple_of(s * R, 16), R), :] = jnp.where(m, 1.0, 0.0).astype(bf16)
        vt = v.T
        cid = lax.broadcasted_iota(jnp.int32, (T, R), 1).astype(f32) + base_row
        o = jnp.zeros((T, R), f32)
        for j in range(8):
            o = o + jnp.where(cid == vt[:, j:j + 1], vt[:, 8 + j:9 + j], 0.0)
        cm[pl.ds(pl.multiple_of(s * T, 16), T), :] = o.astype(bf16)
        return 0

    lax.fori_loop(0, N, tables, 0)
    tick(jnp.int32(2))

    def chunk(c, _):
        for h in range(2):
            wait(xbuf, 4 * T, sb_r.at[2 * c + h])
        for h in range(2):
            for p in range(4):
                r = [dot(dm[(2 * p + q) * R:(2 * p + q + 1) * R, :], xr(2 * c + h, 2 * p + q)[...]) for q in range(2)]
                for e in range(EL):
                    z[h * ROWS + e * EM + p * 80:h * ROWS + e * EM + p * 80 + 80, :] = jnp.concatenate(
                        [r[0][e * SL:(e + 1) * SL], r[1][e * SL:(e + 1) * SL]], axis=0).astype(bf16)

        def one(e, _):
            i = NC + c * EL + e
            @pl.when(e == 0)
            def _():
                tick(2 * c + 3)

            @pl.when(e == 4)
            def _():
                tick(2 * c + 4)
            base = wait_item(i)
            lhs = jnp.concatenate([ld(z, e * EM, EM), ld(z, ROWS + e * EM, EM)], axis=1)
            for t in range(NT):
                r = dot(lhs, ld(w, base + t * KC, KC))
                at = pl.ds(pl.multiple_of(t * ROWS + e * EM, 8), EM)
                acc[at, :] = jnp.where(c > 0, acc[at, :], 0.0) + r
            start_item(i + NSLOT)
            return 0

        lax.fori_loop(0, EL, one, 0)
        return 0

    lax.fori_loop(0, NC, chunk, 0)

    for s in range(NS):
        wait(xbuf, 7 * T, ag_s.at[s])
    for dev in (dx, dy, ds):
        pl.semaphore_signal(ready, inc=1, device_id={"ep": dev}, device_id_type=pl.DeviceIdType.MESH)

    def hid(e, _):
        def put(t, v, n):
            xbuf[pl.ds(pl.multiple_of(t * ROWS + e * EM, 16), EM), 0:n] = v
        hidden(e * EM, EM, put)
        return 0

    lax.fori_loop(0, EL, hid, 0)

    def chip(q):
        return ((mx + q // 2) % 2) * 2 + (my + q % 2) % 2

    def q_at(c, q, h, r0=0, n=T):
        return pl.ds(pl.multiple_of(((c * 4 + q) * 2 + h) * T + r0, 8), n)

    def combine(c):
        slot = c % 2

        @pl.when(c >= 2)
        def _():
            wait(ssend, 2048, sib_s.at[slot])
        for q in range(4):
            s = chip(q) * 2 + (1 - mc)
            cw = ld(cm, s * T, T)
            for h in range(2):
                r = dot(cw, ld(z, h * ROWS + s * R, R))
                ssend[pl.ds(pl.multiple_of(slot * 2048 + (q * 2 + h) * T, T), T), :] = r.astype(bf16)

        @pl.when(c == 0)
        def _():
            pl.semaphore_wait(ready, 3)

        @pl.when(c >= 2)
        def _():
            pl.semaphore_wait(credit, 1)
        for q in range(4):
            s = chip(q) * 2 + mc
            cw = ld(cm, s * T, T)
            for h in range(2):
                acc[q_at(c, q, h), :] = dot(cw, ld(z, h * ROWS + s * R, R))
        send(rows(ssend, slot * 2048, 2048), rows(xbuf, SIBR + slot * 2048, 2048), sib_s.at[slot], sib_r.at[slot], ds)

    def pairs(c):
        slot = c % 2
        wait(xbuf, 2048, sib_r.at[slot])

        @pl.when(c >= 2)
        def _():
            wait(xbuf, 512, s1_s.at[slot])
        sib = SIBR + slot * 2048
        for q in range(4):
            for h in range(2):
                r = acc[q_at(c, q, h), :] + ld(xbuf, sib + (q * 2 + h) * T, T).astype(f32)
                if q < 3:
                    acc[q_at(c, q, h), :] = r
                else:
                    for k in range(2):
                        xbuf[pl.ds(pl.multiple_of(S1S + slot * 512 + (k * 2 + h) * 128, 128), 128), :] = (
                            r[k * 128:(k + 1) * 128].astype(bf16))

        @pl.when(c < NC - 2)
        def _():
            pl.semaphore_signal(credit, inc=1, device_id={"ep": ds}, device_id_type=pl.DeviceIdType.MESH)
        for k, dev in ((0, dx), (1, dy)):
            send(rows(xbuf, S1S + slot * 512 + k * 256, 256), rows(xbuf, S1R + c * 512 + k * 256, 256),
                 s1_s.at[slot], s1_r.at[c], dev)

    def paths(c):
        slot = c % 2
        wait(xbuf, 512, s1_r.at[c])

        @pl.when(c >= 2)
        def _():
            wait(xbuf, 1024, s2_s.at[slot])
        got = S1R + c * 512
        for h in range(2):
            yn = acc[q_at(c, 1, h), :]
            yn = jnp.concatenate([yn[:128] + ld(xbuf, got + h * 128, 128).astype(f32), yn[128:]], axis=0)
            xn = acc[q_at(c, 2, h), :]
            xn = jnp.concatenate([xn[:128], xn[128:] + ld(xbuf, got + 256 + h * 128, 128).astype(f32)], axis=0)
            for k, v in ((0, xn), (1, yn)):
                dm[pl.ds(pl.multiple_of(slot * 1024 + (k * 2 + h) * T, T), T), :] = v.astype(bf16)
        for k, dev in ((0, dx), (1, dy)):
            send(rows(dm, slot * 1024 + k * 512, 512), rows(xbuf, S2R + c * 1024 + k * 512, 512),
                 s2_s.at[slot], s2_r.at[c], dev)

    def result(c):
        wait(xbuf, 1024, s2_r.at[c])

        @pl.when(c >= 1)
        def _():
            wait(dm, 512, ysem)
        got = S2R + c * 1024
        for h in range(2):
            r = acc[q_at(c, 0, h), :] + ld(xbuf, got + h * T, T).astype(f32) + ld(xbuf, got + 512 + h * T, T).astype(f32)
            r = r + ld(acc, SHR + (c * 2 + h) * T, T)
            dm[YST + h * T:YST + (h + 1) * T, :] = r.astype(bf16)
        for h in range(2):
            pltpu.make_async_copy(
                dm.at[pl.ds(YST + h * T, T)],
                y.at[:, pl.ds(pl.multiple_of(c * KC + h * W, W), W)], ysem).start()

    def column(c, _):
        @pl.when((c >= 1) & (c < NC + 1))
        def _():
            pairs(c - 1)

        @pl.when(c < NC)
        def _():
            i = ITEMS1 + c * PER2

            def pair(j, _):
                base = wait_item(i + j)
                for h in range(2):
                    r = []
                    for ee in range(2):
                        e = j * 2 + ee
                        lhs = jnp.concatenate(
                            [ld(xbuf, t * ROWS + e * EM, EM) for t in range(5)]
                            + [xbuf[pl.ds(pl.multiple_of(5 * ROWS + e * EM, 16), EM), 0:128]], axis=1)
                        r.append(dot(lhs, ld(w, base + (ee * 2 + h) * FF, FF)))
                    for s in range(N):
                        z[pl.ds(pl.multiple_of(h * ROWS + s * R + j * 80, 16), 80), :] = jnp.concatenate(
                            [r[0][s * SL:(s + 1) * SL], r[1][s * SL:(s + 1) * SL]], axis=0).astype(bf16)
                start_item(i + j + NSLOT)

                @pl.when((j == 1) & (c >= 2))
                def _():
                    paths(c - 2)
                return 0

            lax.fori_loop(0, 4, pair, 0)
            base = wait_item(i + 4, SLOT // 2)
            for h in range(2):
                acc[pl.ds(pl.multiple_of(SHR + (c * 2 + h) * T, 8), T), :] = dot(hsh[...], ld(w, base + h * FF, FF))
            start_item(i + 4 + NSLOT)
            combine(c)

        @pl.when((c >= NC) & (c < NC + 2))
        def _():
            paths(c - 2)

        @pl.when(c >= 3)
        def _():
            result(c - 3)
        return 0

    lax.fori_loop(0, NC + 3, column, 0)
    wait(dm, 512, ysem)
    for slot in range(2):
        wait(ssend, 2048, sib_s.at[slot])
        wait(xbuf, 512, s1_s.at[slot])
        wait(xbuf, 1024, s2_s.at[slot])


def solution(mesh):
    def step(x, expert, slot, gate, w_gate, w_up, w_down, s_gate, s_up, s_down):
        x = x.reshape(T, D)
        code = jnp.where(slot < SL, expert * SL + slot, -1).reshape(T, 8).astype(f32)
        g = gate.reshape(T, 8).astype(bf16).astype(f32)
        info = jnp.concatenate([code.T, g.T], axis=0)
        hbm, vmem = pl.BlockSpec(memory_space=pl.ANY), pl.BlockSpec(memory_space=pltpu.VMEM)
        dma = pltpu.SemaphoreType.DMA
        y = pl.pallas_call(
            kernel,
            out_shape=jax.ShapeDtypeStruct((T, D), bf16),
            in_specs=[hbm, vmem] + [hbm] * 6,
            out_specs=hbm,
            scratch_shapes=[
                pltpu.VMEM((XROWS, W), bf16),
                pltpu.VMEM((NT * ROWS, W), f32),
                pltpu.VMEM((NSLOT * SLOT, W), bf16),
                pltpu.VMEM((2 * ROWS, W), bf16),
                pltpu.VMEM((N * R, T), bf16),
                pltpu.VMEM((N * T, R), bf16),
                pltpu.VMEM((T, FF), bf16),
                pltpu.VMEM((2 * 2048, W), bf16),
                pltpu.VMEM((N * 16, T), f32),
                dma((NSLOT,)), dma, dma, dma,
                dma((NS,)), dma((NS,)), dma((NS,)), dma((NS,)),
                dma((2,)), dma((2,)), dma((2,)), dma((NC,)), dma((2,)), dma((NC,)), dma,
                pltpu.SemaphoreType.REGULAR, pltpu.SemaphoreType.REGULAR,
            ],
            compiler_params=pltpu.CompilerParams(
                collective_id=0, has_side_effects=True, vmem_limit_bytes=67043328),
        )(x, info, w_gate, w_up, w_down, s_gate, s_up, s_down)
        return y.reshape(1, 1, T, D)

    tok, exp = P("dp", "ep", None, None), P("ep", None, None)
    whole = P(None, None)
    return jax.shard_map(
        step, mesh=mesh,
        in_specs=(tok, tok, tok, tok, exp, exp, exp, whole, whole, whole),
        out_specs=tok, check_vma=False)
```

time: 672 us -> 219 us (0.33)
  blocking collectives: 236 us -> 0 us
  Pallas kernels: 0 us -> 213 us
  matrix products: 205 us -> 0 us
  waiting for transfers between devices: 193 us -> 0 us
  local copies, waits for them, and re-layouts: 31.3 us -> 3.13 us
    another operation x1 -> x0, blocking collectives: 236 us -> none  [placed(): return lax.with_sharding_constraint(v, NamedSharding(mesh, P(*spec)))]
    pallas_call x0 -> x1, Pallas kernels: none -> 213 us  [step(): pl.pallas_call(kernel, out_shape=jax.ShapeDtypeStruct((T, D), bf16), in_s...]
    dot_general x9 -> x0, matrix products: 205 us -> none  [einsum(): return jnp.einsum(form, a.astype(jnp.float32), b.astype(jnp.float32))]
    another operation x1 -> x0, waiting for transfers between devices: 193 us -> none  [placed(): return lax.with_sharding_constraint(v, NamedSharding(mesh, P(*spec)))]
    another operation x1 -> x0, local copies, waits for them, and re-layouts: 17.5 us -> none  [placed(): return lax.with_sharding_constraint(v, NamedSharding(mesh, P(*spec)))]
    convert_element_type x3 -> x0, local copies, waits for them, and re-layouts: 11.4 us -> none  [the longest x1 5.62 us: step(): einsum('abtke,abtkc->abtec', to_expert, to_slot).astype(jnp.bfloat16)]
  transfers between devices with their start and end apart: 1 -> 0, of which waited for: 1 -> 0; matrix products, arithmetic and copies ran while one was open for 5% -> 0% of each run, Pallas kernels for 0% -> 0%
where the time goes in v1:
time: 219 us; the launch traced here: 218 us
  Pallas kernels  213 us (97%)
  local copies, waits for them, and re-layouts  3.13 us (1%)
    pallas_call x1, Pallas kernels, step(): pl.pallas_call(kernel, out_shape=jax.ShapeDtypeStruct((T, D), bf16), in_s...  213 us

profile of v1, /device:TPU:0, one launch (start us, length us, event | category | flops | bytes accessed | tf_op | source)
XLA Modules:
  0.0 218.4 jit_solution(13323684037829564196)
XLA Ops:
  0.0 0.7 convert_bitcast_fusion.1
  0.7 0.7 convert_bitcast_fusion
  1.4 0.6 pad_maximum_fusion.info
  2.0 213.3 %shard_map.100 = bf16[256,4096]{1,0:T(8,128)(2,1)} custom-call(bf16[256,4096]{1,0:T(8,128)(2,1)} %bitcast.12, f32[16,256]{1,0:T(8,128)} %pad_maximum_fusion.info, bf16[8,4096,1408]{2,1,0:T(8,128)(2,1)} %wg.1, bf16[8,4096,1408]{2,1,0:T(8,128)(2,1)} %wu.1, bf16[8,1408,4096]{2,1,0:T(8,128)(2,1)} %wd.1, bf16[4096,1408]{1,0:T(8,128)(2,1)} %sg.1, ...), custom_call_target="tpu_custom_call" | custom-call | tf_op jit(solution)/shard_map/pallas_call | solution.py:414
  215.3 3.1 %copy.12 = bf16[1,1,256,4096]{3,2,1,0:T(8,128)(2,1)} copy(bf16[1,1,256,4096]{3,2,1,0:T(8,128)(2,1)} %bitcast.11) | data formatting | bytes 4194304
